TPU v7x, 32 devices: a whole 2x2x4 slice. The times are simulated.
32 devices in a mesh: row: 8 (over y, x, core), col: 4 (over z).
Axes of the slice: x: 2, y: 2, z: 4, core: 2. Of those that a mesh axis runs over, the one named last changes fastest.
Arguments:
- density: float32 [256, 256, 256], P('row', 'col'), may hold values from -5 to 5
- green_octant: float32 [256, 256, 256], P('row', 'col'), may hold values from 0 to 0.25
Outputs:
- potential: float32 [256, 256, 256], P('row', 'col')
All inputs are finite; a program needn't handle non-finite values.
Results may differ from a plain program's by a relative error of at most 0.000092.
Values sent between devices are 32-bit elements; how exact they have to be, the bound alone decides.
A program may use at most 192 MiB of HBM per device.

v0:
```python
import jax
import jax.numpy as jnp
import numpy as np
from jax import lax
from jax.experimental import pallas as pl
from jax.experimental.pallas import tpu as pltpu
from jax.sharding import PartitionSpec as P

F32 = jnp.float32
BF16 = jnp.bfloat16
VMEM_BYTES = 60 * 1024 * 1024


def trig(extent):
    k = np.arange(extent)[:, None]
    n = np.arange(extent)[None, :]
    phase = ((2 * k + 1) * n) % (4 * extent)
    angle = 2.0 * np.pi * phase / (4 * extent)
    weight = np.where(n == 0, 1.0, 2.0)
    return np.cos(angle), np.sin(angle), weight * np.cos(angle)


def halves(table):
    table = np.asarray(table, np.float32)
    high = table.astype(BF16)
    low = (table - high.astype(np.float32)).astype(BF16)
    return jnp.asarray(np.stack([high, low]))


def split(value):
    high = value.astype(BF16)
    return high, (value - high.astype(F32)).astype(BF16)


def dot3(left, right, dims=((1,), (0,))):
    def one(a, b):
        return lax.dot_general(a, b, (dims, ((), ())), preferred_element_type=F32)

    return one(left[0], right[0]) + (one(left[0], right[1]) + one(left[1], right[0]))


def fused_kernel(sizes, dens_ref, green_ref, wave_ref, even_ref, y_ref, ky_ref, x_ref, kx_ref,
                 xi_ref, yi_ref, back_ref, out_ref, dens_two, green_two, send, recv, bsend, brecv,
                 total, send_sem, recv_sem, bsend_sem, brecv_sem):
    nrow, ncol, groups, per, width, chunks, each, parts = sizes
    ndev = nrow * ncol
    rows = nrow * groups
    cells = dens_ref.shape[0]
    me = lax.axis_index("row") * ncol + lax.axis_index("col")
    size, bsize = each * 3 * groups, each * 2 * groups

    def other(step):
        target = lax.rem(me + step, ndev)
        return target, (lax.div(target, ncol), lax.rem(target, ncol))

    barrier = pltpu.get_barrier_semaphore()

    def greet(step, carry):
        pl.semaphore_signal(
            barrier, inc=1, device_id=other(step)[1], device_id_type=pl.DeviceIdType.MESH
        )
        return carry

    lax.fori_loop(1, ndev, greet, 0)

    def pair(ref):
        return ref[0], ref[1]

    def block(ref, chunk, owner, length):
        start = pl.multiple_of((chunk * ndev + owner) * length, 8)
        return ref.at[pl.ds(start, length), :]

    def spread(source, target, length, chunk, out_sem, in_sem):
        def one(step, carry):
            owner, device = other(step)
            pltpu.make_async_remote_copy(
                src_ref=block(source, chunk, owner, length),
                dst_ref=block(target, chunk, me, length),
                send_sem=out_sem.at[chunk],
                recv_sem=in_sem.at[chunk],
                device_id=device,
                device_id_type=pl.DeviceIdType.MESH,
            ).start()
            return carry

        lax.fori_loop(1, ndev, one, 0)
        block(target, chunk, me, length)[...] = block(source, chunk, me, length)[...]

    def landed(ref, length, chunk, sem):
        start = pl.multiple_of(chunk * ndev * length, 8)
        view = ref.at[pl.ds(start, (ndev - 1) * length), :]
        pltpu.make_async_copy(view, view, sem.at[chunk]).wait()

    for ref, two in ((dens_ref, dens_two), (green_ref, green_two)):
        high, low = split(ref[...])
        two[0] = high
        two[1] = low

    lines = ndev * each
    step_cells = min(256, cells)

    def transform(chunk):
        for two, table, first, count in (
            (dens_two, wave_ref, 0, 2),
            (green_two, even_ref, 2, 1),
        ):
            left = (table[0, chunk], table[1, chunk])
            for begin in range(0, cells, step_cells):
                right = (two[0, begin : begin + step_cells], two[1, begin : begin + step_cells])
                result = dot3(left, right, ((1,), (1,)))
                for part in range(count):
                    for tile in range(step_cells // 128):
                        group = begin // 128 + tile
                        start = chunk * ndev * size + (first + part) * groups + group
                        send[pl.ds(start, lines, stride=3 * groups), :] = result[
                            part * lines : (part + 1) * lines, tile * 128 : (tile + 1) * 128
                        ]

    transform(0)
    pl.semaphore_wait(barrier, ndev - 1)
    spread(send, recv, size, 0, send_sem, recv_sem)

    def forward(chunk, carry):
        transform(chunk)
        spread(send, recv, size, chunk, send_sem, recv_sem)
        return carry

    lax.fori_loop(1, chunks, forward, 0)

    def planes(chunk, carry):
        landed(recv, size, chunk, recv_sem)

        def load(slot, part):
            def piece(r, c):
                start = ((chunk * ndev + r * ncol + c) * each + slot) * 3 * groups + part * groups
                return recv[pl.ds(start, groups), :]

            columns = [
                jnp.concatenate([piece(r, c) for r in range(nrow)], axis=0) for c in range(ncol)
            ]
            return jnp.concatenate(
                [
                    jnp.concatenate([v[:, h * width : (h + 1) * width] for v in columns], axis=1)
                    for h in range(per)
                ],
                axis=0,
            )

        def one_slot(slot, inner):
            green = dot3(split(load(slot, 2)), pair(ky_ref))
            green = dot3(pair(kx_ref), split(green))
            green = jnp.concatenate([green, green], axis=1)
            green = jnp.concatenate([green, green], axis=0)
            for part in range(2):
                value = dot3(split(load(slot, part)), pair(y_ref))
                value = dot3(pair(x_ref), split(value)) * green
                value = dot3(pair(xi_ref), split(value))
                value = dot3(split(value), pair(yi_ref))
                for c in range(ncol):
                    piece = jnp.concatenate(
                        [
                            value[h * rows : (h + 1) * rows, c * width : (c + 1) * width]
                            for h in range(per)
                        ],
                        axis=1,
                    )
                    for r in range(nrow):
                        start = ((chunk * ndev + r * ncol + c) * each + slot) * 2 * groups
                        start = start + part * groups
                        bsend[pl.ds(start, groups), :] = piece[r * groups : (r + 1) * groups]
            return inner

        lax.fori_loop(0, each, one_slot, 0)
        spread(bsend, brecv, bsize, chunk, bsend_sem, brecv_sem)
        return carry

    lax.fori_loop(0, chunks, planes, 0)

    depth = 2 * lines * chunks // parts
    for half in range(parts):
        for chunk in range(half * chunks // parts, (half + 1) * chunks // parts):
            landed(brecv, bsize, chunk, brecv_sem)
        for group in range(groups):
            value = brecv[pl.ds(half * depth * groups + group, depth, stride=groups), :]
            table = (back_ref[0, half], back_ref[1, half])
            result = dot3(table, split(value))
            if half > 0:
                result = result + total[:, group * 128 : (group + 1) * 128]
            if half < parts - 1:
                total[:, group * 128 : (group + 1) * 128] = result
            else:
                out_ref[pl.ds(group * 128, 128), :] = result.T

    def finish(chunk, carry):
        landed(send, size, chunk, send_sem)
        landed(bsend, bsize, chunk, bsend_sem)
        return carry

    lax.fori_loop(0, chunks, finish, 0)


def make(mesh):
    nrow, ncol = mesh.shape["row"], mesh.shape["col"]
    ndev = nrow * ncol

    def on_device(density, green_octant):
        xl, width, extent = density.shape
        slots = extent // ndev
        per = 128 // width
        groups = xl // per
        cells = xl * width
        each = min(2, slots)
        chunks = slots // each
        parts = chunks
        cosine, sine, even = trig(extent)

        def chunked(table):
            return table.reshape(ndev, chunks, each, extent).transpose(1, 0, 2, 3)

        lines = ndev * each
        waves = np.stack([chunked(cosine), chunked(sine)], axis=1).reshape(
            chunks, 2 * lines, extent
        )
        evens = chunked(even).reshape(chunks, lines, extent)
        back = np.stack([chunked(cosine), chunked(sine)], axis=3).reshape(parts, -1, extent)
        back = back.transpose(0, 2, 1)
        both = np.concatenate([cosine, sine], axis=0)
        order = np.arange(extent).reshape(nrow, groups, per).transpose(2, 0, 1).reshape(-1)
        scale = 1.0 / extent
        tables = (
            halves(waves),
            halves(evens),
            halves(both.T),
            halves(even.T),
            halves(both[:, order]),
            halves(even[:, order]),
            halves(both[:, order].T * scale),
            halves(both * scale),
            halves(back * scale),
        )
        operands = (
            density.reshape(cells, extent),
            green_octant.reshape(cells, extent),
        ) + tables
        size, bsize = each * 3 * groups, each * 2 * groups
        sizes = (nrow, ncol, groups, per, width, chunks, each, parts)
        out = pl.pallas_call(
            lambda *refs: fused_kernel(sizes, *refs),
            in_specs=[pl.BlockSpec(memory_space=pltpu.VMEM)] * len(operands),
            out_specs=pl.BlockSpec(memory_space=pltpu.VMEM),
            out_shape=jax.ShapeDtypeStruct((cells, extent), F32),
            scratch_shapes=[
                pltpu.VMEM((2, cells, extent), BF16),
                pltpu.VMEM((2, cells, extent), BF16),
                pltpu.VMEM((chunks * ndev * size, 128), F32),
                pltpu.VMEM((chunks * ndev * size, 128), F32),
                pltpu.VMEM((chunks * ndev * bsize, 128), F32),
                pltpu.VMEM((chunks * ndev * bsize, 128), F32),
                pltpu.VMEM((extent, cells), F32),
            ]
            + [pltpu.SemaphoreType.DMA((chunks,))] * 4,
            compiler_params=pltpu.CompilerParams(
                vmem_limit_bytes=VMEM_BYTES, collective_id=0, has_side_effects=True
            ),
            name="fused",
        )(*operands)
        return out.reshape(xl, width, extent)

    return on_device


def solution(mesh):
    return jax.shard_map(
        make(mesh),
        mesh=mesh,
        in_specs=(P("row", "col", None), P("row", "col", None)),
        out_specs=P("row", "col", None),
        check_vma=False,
    )
```

profile of v0, /device:TPU:9, one launch (start us, length us, event | category | flops | bytes accessed | tf_op | source)
XLA Modules:
  0.0 240.0 jit_solution(1853628449421876386)
XLA Ops:
  0.0 236.9 %fused.1 = f32[2048,256]{1,0:T(8,128)} custom-call(f32[2048,256]{1,0:T(8,128)} %bitcast.4, f32[2048,256]{1,0:T(8,128)} %bitcast.5, bf16[2,4,128,256]{3,2,1,0:T(8,128)(2,1)} %constant.18.clone.refs_2_, bf16[2,4,64,256]{3,2,1,0:T(8,128)(2,1)} %constant.19.clone.refs_3_, bf16[2,256,512]{2,1,0:T(8,128)(2,1)} %constant.20.clone.refs_4_, ...), custom_call_target="tpu_custom_call" | custom-call | tf_op jit(solution)/shard_map/fused/pallas_call | solution.py:247
  236.9 3.1 %copy.13 = f32[32,64,256]{2,1,0:T(8,128)} copy(f32[32,64,256]{2,1,0:T(8,128)} %bitcast.3) | data formatting | bytes 4194304
where the time goes:
time: 242 us; the launch traced here: 240 us
  Pallas kernels  237 us (98%)
  local copies, waits for them, and re-layouts  3.13 us (1%)
    pallas_call x1, Pallas kernels, on_device(): pl.pallas_call(lambda *refs: fused_kernel(sizes, *refs), in_specs=[pl.Blo...  237 us

commit v1 on v0

v1 whole, which is shorter than its diff:
```python
import jax
import jax.numpy as jnp
import numpy as np
from jax import lax
from jax.experimental import pallas as pl
from jax.experimental.pallas import tpu as pltpu
from jax.sharding import PartitionSpec as P

F32 = jnp.float32
BF16 = jnp.bfloat16
VMEM_BYTES = 62 * 1024 * 1024
MESH = pl.DeviceIdType.MESH


def halves(table):
    table = np.asarray(table, np.float32)
    high = table.astype(BF16)
    low = (table - high.astype(np.float32)).astype(BF16)
    return jnp.asarray(np.stack([high, low]))


def split(value):
    high = value.astype(BF16)
    return high, (value - high.astype(F32)).astype(BF16)


def dot(a, b, dims=((1,), (0,))):
    return lax.dot_general(a, b, (dims, ((), ())), preferred_element_type=F32)


def dot3(left, right, dims=((1,), (0,))):
    return dot(left[0], right[0], dims) + (
        dot(left[0], right[1], dims) + dot(left[1], right[0], dims)
    )


def pair(ref):
    return ref[0], ref[1]


def fused_kernel(sizes, dens_ref, green_ref, f_ref, ft_ref, w_ref, wt_ref, fold_ref, out_ref,
                 dens_two, green_two, raw_out, raw_in, far_two, dsend, drecv, gsend, grecv,
                 bsend, brecv, ret_out, ret_in, total, raw_ssem, raw_rsem, d_ssem, d_rsem,
                 g_ssem, g_rsem, b_ssem, b_rsem, ret_ssem, ret_rsem):
    nrow, ncol, groups, per, width, each, blocks = sizes
    cells, extent = dens_ref.shape
    mid = extent // 2
    xl = groups * per
    hc = ncol // 2
    nsets = nrow * ncol
    team = nrow * hc
    chunks = extent // (team * each)
    row, col = lax.axis_index("row"), lax.axis_index("col")
    me = row * ncol + col
    half = lax.div(col, hc)
    away = 1 - half
    spot = col - half * hc
    rank = row * hc + spot
    relay_here = col == hc - 1 + half
    size = each * groups
    bgroups = groups // blocks

    def place(index):
        return lax.div(index, ncol), lax.rem(index, ncol)

    def greet(step, carry):
        pl.semaphore_signal(
            barrier, inc=1, device_id=place(lax.rem(me + step, nsets)), device_id_type=MESH
        )
        return carry

    barrier = pltpu.get_barrier_semaphore()
    lax.fori_loop(1, nsets, greet, 0)

    def remote(source, target, send_sem, recv_sem, device):
        return pltpu.make_async_remote_copy(
            src_ref=source,
            dst_ref=target,
            send_sem=send_sem,
            recv_sem=recv_sem,
            device_id=device,
            device_id_type=MESH,
        )

    def rows(ref, start, length):
        return ref.at[pl.ds(pl.multiple_of(start, 8), length), :]

    def wait(ref, length, sem):
        view = ref.at[pl.ds(0, length), :]
        pltpu.make_async_copy(view, view, sem).wait()

    def fold(g, carry):
        def pick(ref):
            return jnp.concatenate(
                [
                    ref[pl.ds(pl.multiple_of((h * groups + g) * width, width), width), :]
                    for h in range(per)
                ],
                axis=0,
            )

        start = pl.multiple_of(g * 128, 128)
        high, low = split(pick(dens_ref))
        dens_two[0, pl.ds(start, 128), :] = high
        dens_two[1, pl.ds(start, 128), :] = low
        raw_out[pl.ds(start, 128), :] = dot(high, fold_ref[away]) + dot(low, fold_ref[away])
        cell = lax.broadcasted_iota(jnp.int32, (128, extent), 0)
        z = lax.broadcasted_iota(jnp.int32, (128, extent), 1)
        lane_h = lax.div(cell, width)
        y = cell - lane_h * width + col * width
        x = lane_h * groups + g + row * xl
        weight = jnp.where(x == 0, 1.0, 2.0) * jnp.where(y == 0, 1.0, 2.0)
        weight = weight * jnp.where(z == 0, 1.0, 2.0) * (1.0 / (extent * extent * extent))
        high, low = split(pick(green_ref) * weight)
        green_two[0, pl.ds(start, 128), :] = high
        green_two[1, pl.ds(start, 128), :] = low
        return carry

    lax.fori_loop(0, groups, fold, 0)
    pl.semaphore_wait(barrier, nsets - 1)

    far_relay = (row, hc - 1 + away)
    brows = bgroups * 128
    for b in range(blocks):
        part = raw_out.at[pl.ds(b * brows, brows), :]
        remote(
            part, raw_in.at[spot, pl.ds(b * brows, brows), :], raw_ssem.at[b],
            raw_rsem.at[spot, b], far_relay,
        ).start()

    def transform(two, table, send, line):
        def tile(t, carry):
            start = pl.multiple_of(t * 256, 256)
            right = (two[0, pl.ds(start, 256), :], two[1, pl.ds(start, 256), :])
            result = dot3(table, right, ((1,), (1,)))
            for i in range(2):
                send[pl.ds(line * extent * groups + t * 2 + i, extent, stride=groups), :] = (
                    result[:, i * 128 : (i + 1) * 128]
                )
            return carry

        lax.fori_loop(0, cells // 256, tile, 0)

    w_here = (w_ref[half, 0], w_ref[half, 1])
    transform(dens_two, w_here, dsend, 0)

    def scatter_dens(chunk, line, source_set):
        def one(step, carry):
            target = lax.rem(rank + step, team)
            device = (lax.div(target, hc), lax.rem(target, hc) + half * hc)
            remote(
                rows(dsend, (line * extent + (chunk * team + target) * each) * groups, size),
                rows(drecv, (chunk * nsets + source_set) * size, size),
                d_ssem.at[chunk], d_rsem.at[chunk], device,
            ).start()
            return carry

        lax.fori_loop(1, team, one, 0)
        rows(drecv, (chunk * nsets + source_set) * size, size)[...] = rows(
            dsend, (line * extent + (chunk * team + rank) * each) * groups, size
        )[...]

    def scatter_own(chunk, carry):
        scatter_dens(chunk, 0, me)
        return carry

    lax.fori_loop(0, chunks, scatter_own, 0)

    transform(green_two, (ft_ref[0, 0:extent], ft_ref[1, 0:extent]), gsend, 0)

    def scatter_green(chunk, carry):
        def one(step, inner):
            target = lax.rem(me + step, nsets)
            r, c = place(target)
            owner = r * hc + lax.rem(c, hc)
            remote(
                rows(gsend, (chunk * team + owner) * size, size),
                rows(grecv, (chunk * nsets + me) * size, size),
                g_ssem.at[chunk], g_rsem.at[chunk], (r, c),
            ).start()
            return inner

        lax.fori_loop(1, nsets, one, 0)
        rows(grecv, (chunk * nsets + me) * size, size)[...] = rows(
            gsend, (chunk * team + rank) * size, size
        )[...]
        return carry

    lax.fori_loop(0, chunks, scatter_green, 0)

    @pl.when(relay_here)
    def _():
        for t in range(hc):
            for b in range(blocks):
                view = raw_in.at[t, pl.ds(b * brows, brows), :]
                pltpu.make_async_copy(view, view, raw_rsem.at[t, b]).wait()
                high, low = split(view[...])
                far_two[0, pl.ds(b * brows, brows), :] = high
                far_two[1, pl.ds(b * brows, brows), :] = low
            w_far = (w_ref[half, 0, :, 0:mid], w_ref[half, 1, :, 0:mid])
            transform(far_two, w_far, dsend, 1 + t)

            def scatter_far(chunk, carry):
                scatter_dens(chunk, 1 + t, row * ncol + away * hc + t)
                return carry

            lax.fori_loop(0, chunks, scatter_far, 0)

    def planes(chunk, carry):
        @pl.when(relay_here)
        def _():
            wait(drecv, (nsets - 1 - hc) * size, d_rsem.at[chunk])

        @pl.when(jnp.logical_not(relay_here))
        def _():
            wait(drecv, (nsets - 1) * size, d_rsem.at[chunk])

        wait(grecv, (nsets - 1) * size, g_rsem.at[chunk])

        def load(ref, slot):
            def piece(r, c):
                start = ((chunk * nsets + r * ncol + c) * each + slot) * groups
                return ref[pl.ds(start, groups), :]

            columns = [
                jnp.concatenate([piece(r, c) for r in range(nrow)], axis=0) for c in range(ncol)
            ]
            layers = [
                jnp.concatenate([v[:, h * width : (h + 1) * width] for v in columns], axis=1)
                for h in range(per)
            ]
            return jnp.concatenate(
                [v[r * groups : (r + 1) * groups] for r in range(nrow) for v in layers], axis=0
            )

        def one_slot(slot, inner):
            cosine = (f_ref[0, :, 0:extent], f_ref[1, :, 0:extent])
            green = dot3(split(load(grecv, slot)), cosine)
            green = dot3((ft_ref[0, 0:extent], ft_ref[1, 0:extent]), split(green))
            green = jnp.concatenate([green, green], axis=1)
            green = jnp.concatenate([green, green], axis=0)
            value = dot3(split(load(drecv, slot)), pair(f_ref))
            value = dot3(pair(ft_ref), split(value)) * green
            value = dot3(pair(f_ref), split(value))
            value = dot3(split(value), pair(ft_ref))
            for c in range(ncol):
                for r in range(nrow):
                    start = ((chunk * nsets + r * ncol + c) * each + slot) * groups
                    bsend[pl.ds(start, groups), :] = jnp.concatenate(
                        [
                            value[
                                r * xl + h * groups : r * xl + (h + 1) * groups,
                                c * width : (c + 1) * width,
                            ]
                            for h in range(per)
                        ],
                        axis=1,
                    )
            return inner

        lax.fori_loop(0, each, one_slot, 0)

        def back(step, inner):
            target = lax.rem(me + step, nsets)
            r, c = place(target)
            here = lax.div(c, hc) == half
            line = jnp.where(here, 0, 1 + lax.rem(c, hc))
            device = (r, jnp.where(here, c, hc - 1 + half))
            source = rows(bsend, (chunk * nsets + target) * size, size)
            sink = rows(brecv, (line * extent + (chunk * team + rank) * each) * groups, size)
            mine = jnp.logical_and(device[0] == row, device[1] == col)

            @pl.when(mine)
            def _():
                sink[...] = source[...]

            @pl.when(jnp.logical_not(mine))
            def _():
                remote(source, sink, b_ssem.at[chunk], b_rsem.at[chunk], device).start()

            return inner

        lax.fori_loop(0, nsets, back, 0)
        return carry

    lax.fori_loop(0, chunks, planes, 0)

    def settle(chunk, carry):
        @pl.when(relay_here)
        def _():
            wait(brecv, (1 + hc) * (team - 1) * size, b_rsem.at[chunk])

        @pl.when(jnp.logical_not(relay_here))
        def _():
            wait(brecv, (team - 1) * size, b_rsem.at[chunk])

        return carry

    lax.fori_loop(0, chunks, settle, 0)

    def lines(line, group):
        return split(brecv[pl.ds(line * extent * groups + group, extent, stride=groups), :])

    @pl.when(relay_here)
    def _():
        table = (wt_ref[half, 0, 0:mid, :], wt_ref[half, 1, 0:mid, :])

        def far_block(b, carry):
            for t in range(hc):
                def far_group(i, inner):
                    g = b * bgroups + i
                    start = pl.multiple_of(g * mid, 8)
                    ret_out[t, pl.ds(start, mid), :] = dot3(table, lines(1 + t, g))
                    return inner

                lax.fori_loop(0, bgroups, far_group, 0)
                start = pl.multiple_of(b * bgroups * mid, 8)
                remote(
                    ret_out.at[t, pl.ds(start, bgroups * mid), :],
                    ret_in.at[pl.ds(start, bgroups * mid), :],
                    ret_ssem.at[b], ret_rsem.at[b], (row, away * hc + t),
                ).start()
            return carry

        lax.fori_loop(0, blocks, far_block, 0)

    def near_group(g, carry):
        start = pl.multiple_of(g * extent, 8)
        total[pl.ds(start, extent), :] = dot3((wt_ref[half, 0], wt_ref[half, 1]), lines(0, g))
        return carry

    lax.fori_loop(0, groups, near_group, 0)

    def finish(b, carry):
        start = pl.multiple_of(b * bgroups * mid, 8)
        view = ret_in.at[pl.ds(start, bgroups * mid), :]
        pltpu.make_async_copy(view, view, ret_rsem.at[b]).wait()

        def one_group(i, inner):
            g = b * bgroups + i
            high, low = split(ret_in[pl.ds(pl.multiple_of(g * mid, 8), mid), :])
            value = dot(fold_ref[away], high) + dot(fold_ref[away], low)
            value = value + total[pl.ds(pl.multiple_of(g * extent, 8), extent), :]
            value = value.T
            for h in range(per):
                start = pl.multiple_of((h * groups + g) * width, width)
                out_ref[pl.ds(start, width), :] = value[h * width : (h + 1) * width]
            return inner

        lax.fori_loop(0, bgroups, one_group, 0)
        return carry

    lax.fori_loop(0, blocks, finish, 0)

    for b in range(blocks):
        view = raw_out.at[pl.ds(b * brows, brows), :]
        pltpu.make_async_copy(view, view, raw_ssem.at[b]).wait()

    def drain(chunk, carry):
        wait(grecv, (nsets - 1) * size, g_ssem.at[chunk])

        @pl.when(relay_here)
        def _():
            wait(dsend, (1 + hc) * (team - 1) * size, d_ssem.at[chunk])
            wait(bsend, (nsets - 1 - hc) * size, b_ssem.at[chunk])

        @pl.when(jnp.logical_not(relay_here))
        def _():
            wait(dsend, (team - 1) * size, d_ssem.at[chunk])
            wait(bsend, (nsets - 1) * size, b_ssem.at[chunk])

        return carry

    lax.fori_loop(0, chunks, drain, 0)

    @pl.when(relay_here)
    def _():
        for b in range(blocks):
            view = ret_in.at[pl.ds(0, hc * bgroups * mid), :]
            pltpu.make_async_copy(view, view, ret_ssem.at[b]).wait()


def make(mesh):
    nrow, ncol = mesh.shape["row"], mesh.shape["col"]

    def on_device(density, green_octant):
        xl, width, extent = density.shape
        per = 128 // width
        groups = xl // per
        cells = xl * width
        hc = ncol // 2
        team = nrow * hc
        slots = extent // team
        each = min(EACH, slots)
        chunks = slots // each
        blocks = min(4, groups)
        mid = extent // 2
        k = np.arange(extent)[:, None]
        n = np.arange(extent)[None, :]
        theta = np.pi / (2 * extent) * (((2 * k + 1) * n) % (4 * extent))
        both = np.concatenate([np.cos(theta), np.sin(theta)], axis=0)
        shifted = np.pi / (4 * extent) * (((2 * k + 1) * (2 * n + 1 - extent)) % (8 * extent))
        waves = np.stack([np.cos(shifted), np.sin(shifted)])
        flip = np.eye(extent)[:, :mid]
        fold = np.stack([flip + flip[::-1], flip - flip[::-1]])
        tables = (
            halves(both.T),
            halves(both),
            halves(waves).transpose(1, 0, 2, 3),
            halves(waves.transpose(0, 2, 1)).transpose(1, 0, 2, 3),
            jnp.asarray(fold.astype(np.float32).astype(BF16)),
        )
        operands = (
            density.reshape(cells, extent),
            green_octant.reshape(cells, extent),
        ) + tables
        sizes = (nrow, ncol, groups, per, width, each, blocks)
        lot = extent * groups
        dma = pltpu.SemaphoreType.DMA
        out = pl.pallas_call(
            lambda *refs: fused_kernel(sizes, *refs),
            in_specs=[pl.BlockSpec(memory_space=pltpu.VMEM)] * len(operands),
            out_specs=pl.BlockSpec(memory_space=pltpu.VMEM),
            out_shape=jax.ShapeDtypeStruct((cells, extent), F32),
            scratch_shapes=[
                pltpu.VMEM((2, cells, extent), BF16),
                pltpu.VMEM((2, cells, extent), BF16),
                pltpu.VMEM((cells, mid), F32),
                pltpu.VMEM((hc, cells, mid), F32),
                pltpu.VMEM((2, cells, mid), BF16),
                pltpu.VMEM(((1 + hc) * lot, 128), F32),
                pltpu.VMEM((2 * lot, 128), F32),
                pltpu.VMEM((lot, 128), F32),
                pltpu.VMEM((2 * lot, 128), F32),
                pltpu.VMEM((2 * lot, 128), F32),
                pltpu.VMEM(((1 + hc) * lot, 128), F32),
                pltpu.VMEM((hc, groups * mid, 128), F32),
                pltpu.VMEM((groups * mid, 128), F32),
                pltpu.VMEM((groups * extent, 128), F32),
                dma((blocks,)),
                dma((hc, blocks)),
                dma((chunks,)),
                dma((chunks,)),
                dma((chunks,)),
                dma((chunks,)),
                dma((chunks,)),
                dma((chunks,)),
                dma((blocks,)),
                dma((blocks,)),
            ],
            compiler_params=pltpu.CompilerParams(
                vmem_limit_bytes=VMEM_BYTES, collective_id=0, has_side_effects=True
            ),
            name="fused",
        )(*operands)
        return out.reshape(xl, width, extent)

    return on_device


EACH = 4


def solution(mesh):
    return jax.shard_map(
        make(mesh),
        mesh=mesh,
        in_specs=(P("row", "col", None), P("row", "col", None)),
        out_specs=P("row", "col", None),
        check_vma=False,
    )
```

time: 242 us -> 259 us (1.070)
  Pallas kernels: 237 us -> 255 us
    pallas_call x1, Pallas kernels: 237 us -> 255 us  [on_device(): pl.pallas_call(lambda *refs: fused_kernel(sizes, *refs), in_specs=[pl.Blo...]
where the time goes in v1:
time: 259 us; the launch traced here: 258 us
  Pallas kernels  255 us (98%)
  local copies, waits for them, and re-layouts  3.13 us (1%)
    pallas_call x1, Pallas kernels, on_device(): pl.pallas_call(lambda *refs: fused_kernel(sizes, *refs), in_specs=[pl.Blo...  255 us

profile of v1, /device:TPU:9, one launch (start us, length us, event | category | flops | bytes accessed | tf_op | source)
XLA Modules:
  0.0 257.9 jit_solution(15980668649323853830)
XLA Ops:
  0.0 254.8 %fused.1 = f32[2048,256]{1,0:T(8,128)} custom-call(f32[2048,256]{1,0:T(8,128)} %bitcast.4, f32[2048,256]{1,0:T(8,128)} %bitcast.5, bf16[2,256,512]{2,1,0:T(8,128)(2,1)} %constant.10.clone.refs_2_, bf16[2,512,256]{2,1,0:T(8,128)(2,1)} %constant.11.clone.refs_3_, bf16[2,2,256,256]{3,2,1,0:T(8,128)(2,1)} %constant.15.refs_4_, ...), custom_call_target="tpu_custom_call" | custom-call | tf_op jit(solution)/shard_map/fused/pallas_call | solution.py:420
  254.8 3.1 %copy.9 = f32[32,64,256]{2,1,0:T(8,128)} copy(f32[32,64,256]{2,1,0:T(8,128)} %bitcast.3) | data formatting | bytes 4194304

commit v2 on v1

--- a/solution.py
+++ b/solution.py
@@ -38,12 +38,13 @@
     return ref[0], ref[1]
 
 
-def fused_kernel(sizes, dens_ref, green_ref, f_ref, ft_ref, w_ref, wt_ref, fold_ref, out_ref,
+def fused_kernel(sizes, dens_hbm, green_hbm, f_hbm, ft_hbm, w_hbm, wt_hbm, fold_hbm, out_hbm,
+                 dens_in, green_in, f_ref, ft_ref, w_ref, wt_ref, fold_ref, out_ref,
                  dens_two, green_two, raw_out, raw_in, far_two, dsend, drecv, gsend, grecv,
-                 bsend, brecv, ret_out, ret_in, total, raw_ssem, raw_rsem, d_ssem, d_rsem,
-                 g_ssem, g_rsem, b_ssem, b_rsem, ret_ssem, ret_rsem):
+                 bsend, brecv, ret_out, ret_in, total, in_sem, dens_sem, out_sem, raw_ssem,
+                 raw_rsem, d_ssem, d_rsem, g_ssem, g_rsem, b_ssem, b_rsem, ret_ssem, ret_rsem, n_ssem, n_rsem):
     nrow, ncol, groups, per, width, each, blocks = sizes
-    cells, extent = dens_ref.shape
+    cells, extent = dens_in.shape
     mid = extent // 2
     xl = groups * per
     hc = ncol // 2
@@ -59,6 +60,7 @@
     relay_here = col == hc - 1 + half
     size = each * groups
     bgroups = groups // blocks
+    brows = bgroups * 128
 
     def place(index):
         return lax.div(index, ncol), lax.rem(index, ncol)
@@ -71,6 +73,37 @@
 
     barrier = pltpu.get_barrier_semaphore()
     lax.fori_loop(1, nsets, greet, 0)
+
+    def strip(ref, b, h):
+        start = (h * groups + b * bgroups) * width
+        return ref.at[pl.ds(start, bgroups * width), :]
+
+    dens_copies = [
+        [
+            pltpu.make_async_copy(strip(dens_hbm, b, h), strip(dens_in, b, h), dens_sem.at[b, h])
+            for h in range(per)
+        ]
+        for b in range(blocks)
+    ]
+    copies = [
+        pltpu.make_async_copy(source, target, in_sem.at[i])
+        for i, (source, target) in enumerate(
+            (
+                (fold_hbm, fold_ref),
+                (w_hbm, w_ref),
+                (green_hbm, green_in),
+                (ft_hbm, ft_ref),
+                (f_hbm, f_ref),
+                (wt_hbm, wt_ref),
+            )
+        )
+    ]
+    copies[0].start()
+    for b in range(blocks):
+        for copy in dens_copies[b]:
+            copy.start()
+    for copy in copies[1:]:
+        copy.start()
 
     def remote(source, target, send_sem, recv_sem, device):
         return pltpu.make_async_remote_copy(
@@ -89,43 +122,33 @@
         view = ref.at[pl.ds(0, length), :]
         pltpu.make_async_copy(view, view, sem).wait()
 
+    def pick(ref, g):
+        return jnp.concatenate(
+            [
+                ref[pl.ds(pl.multiple_of((h * groups + g) * width, width), width), :]
+                for h in range(per)
+            ],
+            axis=0,
+        )
+
     def fold(g, carry):
-        def pick(ref):
-            return jnp.concatenate(
-                [
-                    ref[pl.ds(pl.multiple_of((h * groups + g) * width, width), width), :]
-                    for h in range(per)
-                ],
-                axis=0,
-            )
-
         start = pl.multiple_of(g * 128, 128)
-        high, low = split(pick(dens_ref))
+        high, low = split(pick(dens_in, g))
         dens_two[0, pl.ds(start, 128), :] = high
         dens_two[1, pl.ds(start, 128), :] = low
         raw_out[pl.ds(start, 128), :] = dot(high, fold_ref[away]) + dot(low, fold_ref[away])
-        cell = lax.broadcasted_iota(jnp.int32, (128, extent), 0)
-        z = lax.broadcasted_iota(jnp.int32, (128, extent), 1)
-        lane_h = lax.div(cell, width)
-        y = cell - lane_h * width + col * width
-        x = lane_h * groups + g + row * xl
-        weight = jnp.where(x == 0, 1.0, 2.0) * jnp.where(y == 0, 1.0, 2.0)
-        weight = weight * jnp.where(z == 0, 1.0, 2.0) * (1.0 / (extent * extent * extent))
-        high, low = split(pick(green_ref) * weight)
-        green_two[0, pl.ds(start, 128), :] = high
-        green_two[1, pl.ds(start, 128), :] = low
-        return carry
-
-    lax.fori_loop(0, groups, fold, 0)
-    pl.semaphore_wait(barrier, nsets - 1)
-
-    far_relay = (row, hc - 1 + away)
-    brows = bgroups * 128
+        return carry
+
+    copies[0].wait()
     for b in range(blocks):
-        part = raw_out.at[pl.ds(b * brows, brows), :]
+        for copy in dens_copies[b]:
+            copy.wait()
+        lax.fori_loop(b * bgroups, (b + 1) * bgroups, fold, 0)
+        if b == 0:
+            pl.semaphore_wait(barrier, nsets - 1)
         remote(
-            part, raw_in.at[spot, pl.ds(b * brows, brows), :], raw_ssem.at[b],
-            raw_rsem.at[spot, b], far_relay,
+            rows(raw_out, b * brows, brows), rows(raw_in.at[spot], b * brows, brows),
+            raw_ssem.at[b], raw_rsem.at[spot, b], (row, hc - 1 + away),
         ).start()
 
     def transform(two, table, send, line):
@@ -141,31 +164,52 @@
 
         lax.fori_loop(0, cells // 256, tile, 0)
 
-    w_here = (w_ref[half, 0], w_ref[half, 1])
-    transform(dens_two, w_here, dsend, 0)
-
-    def scatter_dens(chunk, line, source_set):
-        def one(step, carry):
-            target = lax.rem(rank + step, team)
-            device = (lax.div(target, hc), lax.rem(target, hc) + half * hc)
-            remote(
-                rows(dsend, (line * extent + (chunk * team + target) * each) * groups, size),
-                rows(drecv, (chunk * nsets + source_set) * size, size),
-                d_ssem.at[chunk], d_rsem.at[chunk], device,
-            ).start()
-            return carry
-
-        lax.fori_loop(1, team, one, 0)
-        rows(drecv, (chunk * nsets + source_set) * size, size)[...] = rows(
-            dsend, (line * extent + (chunk * team + rank) * each) * groups, size
-        )[...]
-
-    def scatter_own(chunk, carry):
-        scatter_dens(chunk, 0, me)
-        return carry
-
-    lax.fori_loop(0, chunks, scatter_own, 0)
-
+    copies[1].wait()
+    transform(dens_two, (w_ref[half, 0], w_ref[half, 1]), dsend, 0)
+
+    def scatter_dens(lines_sets):
+        def one_chunk(chunk, outer):
+            def one(step, carry):
+                target = lax.rem(rank + step, team)
+                device = (lax.div(target, hc), lax.rem(target, hc) + half * hc)
+                for line, sets in lines_sets:
+                    remote(
+                        rows(
+                            dsend, (line * extent + (chunk * team + target) * each) * groups, size
+                        ),
+                        rows(drecv, (chunk * nsets + sets) * size, size),
+                        d_ssem.at[chunk], d_rsem.at[chunk], device,
+                    ).start()
+                return carry
+
+            lax.fori_loop(1, team, one, 0)
+            for line, sets in lines_sets:
+                rows(drecv, (chunk * nsets + sets) * size, size)[...] = rows(
+                    dsend, (line * extent + (chunk * team + rank) * each) * groups, size
+                )[...]
+            return outer
+
+        lax.fori_loop(0, chunks, one_chunk, 0)
+
+    scatter_dens([(0, me)])
+
+    def weigh(g, carry):
+        cell = lax.broadcasted_iota(jnp.int32, (128, extent), 0)
+        z = lax.broadcasted_iota(jnp.int32, (128, extent), 1)
+        lane_h = lax.div(cell, width)
+        y = cell - lane_h * width + col * width
+        x = lane_h * groups + g + row * xl
+        weight = jnp.where(x == 0, 1.0, 2.0) * jnp.where(y == 0, 1.0, 2.0)
+        weight = weight * jnp.where(z == 0, 1.0, 2.0) * (1.0 / (extent * extent * extent))
+        start = pl.multiple_of(g * 128, 128)
+        high, low = split(pick(green_in, g) * weight)
+        green_two[0, pl.ds(start, 128), :] = high
+        green_two[1, pl.ds(start, 128), :] = low
+        return carry
+
+    copies[2].wait()
+    copies[3].wait()
+    lax.fori_loop(0, groups, weigh, 0)
     transform(green_two, (ft_ref[0, 0:extent], ft_ref[1, 0:extent]), gsend, 0)
 
     def scatter_green(chunk, carry):
@@ -187,24 +231,21 @@
         return carry
 
     lax.fori_loop(0, chunks, scatter_green, 0)
+    copies[4].wait()
+    copies[5].wait()
 
     @pl.when(relay_here)
     def _():
         for t in range(hc):
             for b in range(blocks):
-                view = raw_in.at[t, pl.ds(b * brows, brows), :]
+                view = rows(raw_in.at[t], b * brows, brows)
                 pltpu.make_async_copy(view, view, raw_rsem.at[t, b]).wait()
                 high, low = split(view[...])
                 far_two[0, pl.ds(b * brows, brows), :] = high
                 far_two[1, pl.ds(b * brows, brows), :] = low
             w_far = (w_ref[half, 0, :, 0:mid], w_ref[half, 1, :, 0:mid])
             transform(far_two, w_far, dsend, 1 + t)
-
-            def scatter_far(chunk, carry):
-                scatter_dens(chunk, 1 + t, row * ncol + away * hc + t)
-                return carry
-
-            lax.fori_loop(0, chunks, scatter_far, 0)
+        scatter_dens([(1 + t, row * ncol + away * hc + t) for t in range(hc)])
 
     def planes(chunk, carry):
         @pl.when(relay_here)
@@ -261,69 +302,79 @@
         lax.fori_loop(0, each, one_slot, 0)
 
         def back(step, inner):
-            target = lax.rem(me + step, nsets)
-            r, c = place(target)
-            here = lax.div(c, hc) == half
-            line = jnp.where(here, 0, 1 + lax.rem(c, hc))
-            device = (r, jnp.where(here, c, hc - 1 + half))
-            source = rows(bsend, (chunk * nsets + target) * size, size)
-            sink = rows(brecv, (line * extent + (chunk * team + rank) * each) * groups, size)
-            mine = jnp.logical_and(device[0] == row, device[1] == col)
-
-            @pl.when(mine)
-            def _():
-                sink[...] = source[...]
-
-            @pl.when(jnp.logical_not(mine))
-            def _():
-                remote(source, sink, b_ssem.at[chunk], b_rsem.at[chunk], device).start()
+            r = lax.rem(row + step, nrow)
+            mine = jnp.logical_and(relay_here, r == row)
+            for t in range(hc):
+                source = rows(bsend, (chunk * nsets + r * ncol + away * hc + t) * size, size)
+                start = ((1 + t) * extent + (chunk * team + rank) * each) * groups
+                sink = rows(brecv, start, size)
+
+                @pl.when(mine)
+                def _():
+                    sink[...] = source[...]
+
+                @pl.when(jnp.logical_not(mine))
+                def _():
+                    remote(
+                        source, sink, b_ssem.at[chunk], b_rsem.at[chunk], (r, hc - 1 + half)
+                    ).start()
 
             return inner
 
-        lax.fori_loop(0, nsets, back, 0)
+        lax.fori_loop(0, nrow, back, 0)
         return carry
 
     lax.fori_loop(0, chunks, planes, 0)
 
-    def settle(chunk, carry):
-        @pl.when(relay_here)
-        def _():
-            wait(brecv, (1 + hc) * (team - 1) * size, b_rsem.at[chunk])
-
-        @pl.when(jnp.logical_not(relay_here))
-        def _():
-            wait(brecv, (team - 1) * size, b_rsem.at[chunk])
-
-        return carry
-
-    lax.fori_loop(0, chunks, settle, 0)
+    def near_back(chunk, carry):
+        sink = rows(brecv, (chunk * team + rank) * size, size)
+
+        def one(step, inner):
+            target = lax.rem(rank + step, team)
+            r, c = lax.div(target, hc), lax.rem(target, hc) + half * hc
+            source = rows(bsend, (chunk * nsets + r * ncol + c) * size, size)
+            remote(source, sink, n_ssem.at[0], n_rsem.at[0], (r, c)).start()
+            return inner
+
+        lax.fori_loop(1, team, one, 0)
+        sink[...] = rows(bsend, (chunk * nsets + me) * size, size)[...]
+        return carry
+
+    lax.fori_loop(0, chunks, near_back, 0)
 
     def lines(line, group):
         return split(brecv[pl.ds(line * extent * groups + group, extent, stride=groups), :])
 
+    far_table = (wt_ref[half, 0, 0:mid, :], wt_ref[half, 1, 0:mid, :])
+
     @pl.when(relay_here)
     def _():
-        table = (wt_ref[half, 0, 0:mid, :], wt_ref[half, 1, 0:mid, :])
+        def settle(chunk, carry):
+            wait(brecv, hc * (team - 1) * size, b_rsem.at[chunk])
+            return carry
+
+        lax.fori_loop(0, chunks, settle, 0)
 
         def far_block(b, carry):
             for t in range(hc):
                 def far_group(i, inner):
                     g = b * bgroups + i
                     start = pl.multiple_of(g * mid, 8)
-                    ret_out[t, pl.ds(start, mid), :] = dot3(table, lines(1 + t, g))
+                    ret_out[t, pl.ds(start, mid), :] = dot3(far_table, lines(1 + t, g))
                     return inner
 
                 lax.fori_loop(0, bgroups, far_group, 0)
-                start = pl.multiple_of(b * bgroups * mid, 8)
                 remote(
-                    ret_out.at[t, pl.ds(start, bgroups * mid), :],
-                    ret_in.at[pl.ds(start, bgroups * mid), :],
+                    rows(ret_out.at[t], b * bgroups * mid, bgroups * mid),
+                    rows(ret_in, b * bgroups * mid, bgroups * mid),
                     ret_ssem.at[b], ret_rsem.at[b], (row, away * hc + t),
                 ).start()
             return carry
 
         lax.fori_loop(0, blocks, far_block, 0)
 
+    wait(brecv, (team - 1) * chunks * size, n_rsem.at[0])
+
     def near_group(g, carry):
         start = pl.multiple_of(g * extent, 8)
         total[pl.ds(start, extent), :] = dot3((wt_ref[half, 0], wt_ref[half, 1]), lines(0, g))
@@ -331,13 +382,18 @@
 
     lax.fori_loop(0, groups, near_group, 0)
 
-    def finish(b, carry):
-        start = pl.multiple_of(b * bgroups * mid, 8)
-        view = ret_in.at[pl.ds(start, bgroups * mid), :]
+    out_copies = [
+        [
+            pltpu.make_async_copy(strip(out_ref, b, h), strip(out_hbm, b, h), out_sem.at[b, h])
+            for h in range(per)
+        ]
+        for b in range(blocks)
+    ]
+    for b in range(blocks):
+        view = rows(ret_in, b * bgroups * mid, bgroups * mid)
         pltpu.make_async_copy(view, view, ret_rsem.at[b]).wait()
 
-        def one_group(i, inner):
-            g = b * bgroups + i
+        def one_group(g, inner):
             high, low = split(ret_in[pl.ds(pl.multiple_of(g * mid, 8), mid), :])
             value = dot(fold_ref[away], high) + dot(fold_ref[away], low)
             value = value + total[pl.ds(pl.multiple_of(g * extent, 8), extent), :]
@@ -347,14 +403,19 @@
                 out_ref[pl.ds(start, width), :] = value[h * width : (h + 1) * width]
             return inner
 
-        lax.fori_loop(0, bgroups, one_group, 0)
-        return carry
-
-    lax.fori_loop(0, blocks, finish, 0)
+        lax.fori_loop(b * bgroups, (b + 1) * bgroups, one_group, 0)
+        for copy in out_copies[b]:
+            copy.start()
 
     for b in range(blocks):
-        view = raw_out.at[pl.ds(b * brows, brows), :]
-        pltpu.make_async_copy(view, view, raw_ssem.at[b]).wait()
+        wait(raw_out, brows, raw_ssem.at[b])
+
+    wait(brecv, (team - 1) * chunks * size, n_ssem.at[0])
+
+    @pl.when(relay_here)
+    def _():
+        for b in range(blocks):
+            wait(raw_out, hc * bgroups * mid, ret_ssem.at[b])
 
     def drain(chunk, carry):
         wait(grecv, (nsets - 1) * size, g_ssem.at[chunk])
@@ -362,22 +423,19 @@
         @pl.when(relay_here)
         def _():
             wait(dsend, (1 + hc) * (team - 1) * size, d_ssem.at[chunk])
-            wait(bsend, (nsets - 1 - hc) * size, b_ssem.at[chunk])
+            wait(bsend, hc * (nrow - 1) * size, b_ssem.at[chunk])
 
         @pl.when(jnp.logical_not(relay_here))
         def _():
             wait(dsend, (team - 1) * size, d_ssem.at[chunk])
-            wait(bsend, (nsets - 1) * size, b_ssem.at[chunk])
+            wait(bsend, hc * nrow * size, b_ssem.at[chunk])
 
         return carry
 
     lax.fori_loop(0, chunks, drain, 0)
-
-    @pl.when(relay_here)
-    def _():
-        for b in range(blocks):
-            view = ret_in.at[pl.ds(0, hc * bgroups * mid), :]
-            pltpu.make_async_copy(view, view, ret_ssem.at[b]).wait()
+    for b in range(blocks):
+        for copy in out_copies[b]:
+            copy.wait()
 
 
 def make(mesh):
@@ -393,7 +451,7 @@
         slots = extent // team
         each = min(EACH, slots)
         chunks = slots // each
-        blocks = min(4, groups)
+        blocks = min(BLOCKS, groups)
         mid = extent // 2
         k = np.arange(extent)[:, None]
         n = np.arange(extent)[None, :]
@@ -417,12 +475,15 @@
         sizes = (nrow, ncol, groups, per, width, each, blocks)
         lot = extent * groups
         dma = pltpu.SemaphoreType.DMA
+        any_space = pl.BlockSpec(memory_space=pl.ANY)
         out = pl.pallas_call(
             lambda *refs: fused_kernel(sizes, *refs),
-            in_specs=[pl.BlockSpec(memory_space=pltpu.VMEM)] * len(operands),
-            out_specs=pl.BlockSpec(memory_space=pltpu.VMEM),
+            in_specs=[any_space] * len(operands),
+            out_specs=any_space,
             out_shape=jax.ShapeDtypeStruct((cells, extent), F32),
-            scratch_shapes=[
+            scratch_shapes=[pltpu.VMEM(v.shape, v.dtype) for v in operands]
+            + [
+                pltpu.VMEM((cells, extent), F32),
                 pltpu.VMEM((2, cells, extent), BF16),
                 pltpu.VMEM((2, cells, extent), BF16),
                 pltpu.VMEM((cells, mid), F32),
@@ -437,17 +498,15 @@
                 pltpu.VMEM((hc, groups * mid, 128), F32),
                 pltpu.VMEM((groups * mid, 128), F32),
                 pltpu.VMEM((groups * extent, 128), F32),
+                dma((6,)),
+                dma((blocks, per)),
+                dma((blocks, per)),
                 dma((blocks,)),
                 dma((hc, blocks)),
-                dma((chunks,)),
-                dma((chunks,)),
-                dma((chunks,)),
-                dma((chunks,)),
-                dma((chunks,)),
-                dma((chunks,)),
-                dma((blocks,)),
-                dma((blocks,)),
-            ],
+            ]
+            + [dma((chunks,))] * 6
+            + [dma((blocks,))] * 2
+            + [dma((1,))] * 2,
             compiler_params=pltpu.CompilerParams(
                 vmem_limit_bytes=VMEM_BYTES, collective_id=0, has_side_effects=True
             ),
@@ -458,7 +517,8 @@
     return on_device
 
 
-EACH = 4
+EACH = 2
+BLOCKS = 8
 
 
 def solution(mesh):

time: 259 us -> 218 us (0.84)
  Pallas kernels: 255 us -> 214 us
    pallas_call x1, Pallas kernels: 255 us -> 214 us  [on_device(): pl.pallas_call(lambda *refs: fused_kernel(sizes, *refs), in_specs=[any_sp...]
where the time goes in v2:
time: 218 us; the launch traced here: 217 us
  Pallas kernels  214 us (98%)
  local copies, waits for them, and re-layouts  3.13 us (1%)
    pallas_call x1, Pallas kernels, on_device(): pl.pallas_call(lambda *refs: fused_kernel(sizes, *refs), in_specs=[any_sp...  214 us

profile of v2, /device:TPU:9, one launch (start us, length us, event | category | flops | bytes accessed | tf_op | source)
XLA Modules:
  0.0 217.4 jit_solution(217940175608221922)
XLA Ops:
  0.0 214.3 %fused.1 = f32[2048,256]{1,0:T(8,128)} custom-call(f32[2048,256]{1,0:T(8,128)} %bitcast.4, f32[2048,256]{1,0:T(8,128)} %bitcast.5, bf16[2,256,512]{2,1,0:T(8,128)(2,1)} %constant.10.clone.refs_2_, bf16[2,512,256]{2,1,0:T(8,128)(2,1)} %constant.11.clone.refs_3_, bf16[2,2,256,256]{3,2,1,0:T(8,128)(2,1)} %constant.15.refs_4_, ...), custom_call_target="tpu_custom_call" | custom-call | tf_op jit(solution)/shard_map/fused/pallas_call | solution.py:479
  214.3 3.1 %copy.9 = f32[32,64,256]{2,1,0:T(8,128)} copy(f32[32,64,256]{2,1,0:T(8,128)} %bitcast.3) | data formatting | bytes 4194304

commit v3 on v2

--- a/solution.py
+++ b/solution.py
@@ -42,7 +42,8 @@
                  dens_in, green_in, f_ref, ft_ref, w_ref, wt_ref, fold_ref, out_ref,
                  dens_two, green_two, raw_out, raw_in, far_two, dsend, drecv, gsend, grecv,
                  bsend, brecv, ret_out, ret_in, total, in_sem, dens_sem, out_sem, raw_ssem,
-                 raw_rsem, d_ssem, d_rsem, g_ssem, g_rsem, b_ssem, b_rsem, ret_ssem, ret_rsem, n_ssem, n_rsem):
+                 raw_rsem, d_ssem, d_rsem, g_ssem, g_rsem, b_ssem, b_rsem, ret_ssem, ret_rsem, n_ssem, n_rsem,
+                 o_rsem):
     nrow, ncol, groups, per, width, each, blocks = sizes
     cells, extent = dens_in.shape
     mid = extent // 2
@@ -57,7 +58,9 @@
     away = 1 - half
     spot = col - half * hc
     rank = row * hc + spot
-    relay_here = col == hc - 1 + half
+    relay_spot = (hc - 1) * away
+    relay_here = spot == relay_spot
+    outer = nrow * (hc - 1)
     size = each * groups
     bgroups = groups // blocks
     brows = bgroups * 128
@@ -212,25 +215,85 @@
     lax.fori_loop(0, groups, weigh, 0)
     transform(green_two, (ft_ref[0, 0:extent], ft_ref[1, 0:extent]), gsend, 0)
 
-    def scatter_green(chunk, carry):
+    def green_to(chunk, r, s, side, sem):
+        remote(
+            rows(gsend, (chunk * team + r * hc + s) * size, size),
+            rows(grecv, (chunk * nsets + me) * size, size),
+            g_ssem.at[chunk], sem.at[chunk], (r, s + side * hc),
+        ).start()
+
+    def green_inside(chunk, carry):
         def one(step, inner):
-            target = lax.rem(me + step, nsets)
-            r, c = place(target)
-            owner = r * hc + lax.rem(c, hc)
-            remote(
-                rows(gsend, (chunk * team + owner) * size, size),
-                rows(grecv, (chunk * nsets + me) * size, size),
-                g_ssem.at[chunk], g_rsem.at[chunk], (r, c),
-            ).start()
+            target = lax.rem(rank + step, team)
+            r, s = lax.div(target, hc), lax.rem(target, hc)
+            via = jnp.logical_and(jnp.logical_not(relay_here), s == relay_spot)
+
+            @pl.when(via)
+            def _():
+                green_to(chunk, r, s, half, o_rsem)
+
+            @pl.when(jnp.logical_not(via))
+            def _():
+                green_to(chunk, r, s, half, g_rsem)
+
             return inner
 
-        lax.fori_loop(1, nsets, one, 0)
+        lax.fori_loop(1, team, one, 0)
         rows(grecv, (chunk * nsets + me) * size, size)[...] = rows(
             gsend, (chunk * team + rank) * size, size
         )[...]
         return carry
 
-    lax.fori_loop(0, chunks, scatter_green, 0)
+    def green_away(chunk, carry):
+        def one(step, inner):
+            target = lax.rem(rank + step, team)
+            r, s = lax.div(target, hc), lax.rem(target, hc)
+
+            @pl.when(jnp.logical_or(relay_here, s != relay_spot))
+            def _():
+                green_to(chunk, r, s, away, g_rsem)
+
+            return inner
+
+        lax.fori_loop(0, team, one, 0)
+        return carry
+
+    def hand_on(chunk):
+        wait(grecv, outer * size, o_rsem.at[chunk])
+        for i in range(hc - 1):
+            s = i + lax.convert_element_type(relay_spot <= i, jnp.int32)
+
+            def one(r, inner):
+                block = rows(grecv, (chunk * nsets + r * ncol + half * hc + s) * size, size)
+                remote(
+                    block, block, g_ssem.at[chunk], g_rsem.at[chunk],
+                    (row, away * hc + relay_spot),
+                ).start()
+                return inner
+
+            lax.fori_loop(0, nrow, one, 0)
+
+    def pace(chunk):
+        @pl.when(jnp.logical_and(relay_here, chunk < chunks))
+        def _():
+            hand_on(chunk)
+
+        @pl.when(jnp.logical_and(relay_here, chunk + LEAD < chunks))
+        def _():
+            green_away(chunk + LEAD, 0)
+
+    lead = jnp.where(relay_here, min(LEAD, chunks), chunks)
+
+    def green_first(chunk, carry):
+        green_inside(chunk, 0)
+
+        @pl.when(chunk < lead)
+        def _():
+            green_away(chunk, 0)
+
+        return carry
+
+    lax.fori_loop(0, chunks, green_first, 0)
     copies[4].wait()
     copies[5].wait()
 
@@ -247,16 +310,20 @@
             transform(far_two, w_far, dsend, 1 + t)
         scatter_dens([(1 + t, row * ncol + away * hc + t) for t in range(hc)])
 
+    pace(0)
+
     def planes(chunk, carry):
+        pace(chunk + 1)
+
         @pl.when(relay_here)
         def _():
             wait(drecv, (nsets - 1 - hc) * size, d_rsem.at[chunk])
+            wait(grecv, (nsets - 1 - outer) * size, g_rsem.at[chunk])
 
         @pl.when(jnp.logical_not(relay_here))
         def _():
             wait(drecv, (nsets - 1) * size, d_rsem.at[chunk])
-
-        wait(grecv, (nsets - 1) * size, g_rsem.at[chunk])
+            wait(grecv, (nsets - 1) * size, g_rsem.at[chunk])
 
         def load(ref, slot):
             def piece(r, c):
@@ -418,15 +485,15 @@
             wait(raw_out, hc * bgroups * mid, ret_ssem.at[b])
 
     def drain(chunk, carry):
-        wait(grecv, (nsets - 1) * size, g_ssem.at[chunk])
-
         @pl.when(relay_here)
         def _():
+            wait(drecv, (nsets - 1 + outer) * size, g_ssem.at[chunk])
             wait(dsend, (1 + hc) * (team - 1) * size, d_ssem.at[chunk])
             wait(bsend, hc * (nrow - 1) * size, b_ssem.at[chunk])
 
         @pl.when(jnp.logical_not(relay_here))
         def _():
+            wait(drecv, (nsets - 1 - nrow) * size, g_ssem.at[chunk])
             wait(dsend, (team - 1) * size, d_ssem.at[chunk])
             wait(bsend, hc * nrow * size, b_ssem.at[chunk])
 
@@ -506,7 +573,8 @@
             ]
             + [dma((chunks,))] * 6
             + [dma((blocks,))] * 2
-            + [dma((1,))] * 2,
+            + [dma((1,))] * 2
+            + [dma((chunks,))],
             compiler_params=pltpu.CompilerParams(
                 vmem_limit_bytes=VMEM_BYTES, collective_id=0, has_side_effects=True
             ),
@@ -519,6 +587,7 @@
 
 EACH = 2
 BLOCKS = 8
+LEAD = 2
 
 
 def solution(mesh):

time: 218 us -> 213 us (0.977)
  Pallas kernels: 214 us -> 210 us
    pallas_call x1, Pallas kernels: 214 us -> 210 us  [on_device(): pl.pallas_call(lambda *refs: fused_kernel(sizes, *refs), in_specs=[any_sp...]
where the time goes in v3:
time: 213 us
  Pallas kernels  210 us (99%)
  local copies, waits for them, and re-layouts  3.13 us (1%)
    pallas_call x1, Pallas kernels, on_device(): pl.pallas_call(lambda *refs: fused_kernel(sizes, *refs), in_specs=[any_sp...  210 us

profile of v3, /device:TPU:9, one launch (start us, length us, event | category | flops | bytes accessed | tf_op | source)
XLA Modules:
  0.0 213.1 jit_solution(14147815585438264328)
XLA Ops:
  0.0 209.9 %fused.1 = f32[2048,256]{1,0:T(8,128)} custom-call(f32[2048,256]{1,0:T(8,128)} %bitcast.4, f32[2048,256]{1,0:T(8,128)} %bitcast.5, bf16[2,256,512]{2,1,0:T(8,128)(2,1)} %constant.10.clone.refs_2_, bf16[2,512,256]{2,1,0:T(8,128)(2,1)} %constant.11.clone.refs_3_, bf16[2,2,256,256]{3,2,1,0:T(8,128)(2,1)} %constant.15.refs_4_, ...), custom_call_target="tpu_custom_call" | custom-call | tf_op jit(solution)/shard_map/fused/pallas_call | solution.py:546
  209.9 3.1 %copy.9 = f32[32,64,256]{2,1,0:T(8,128)} copy(f32[32,64,256]{2,1,0:T(8,128)} %bitcast.3) | data formatting | bytes 4194304

commit v4 on v3

--- a/solution.py
+++ b/solution.py
@@ -516,7 +516,7 @@
         hc = ncol // 2
         team = nrow * hc
         slots = extent // team
-        each = min(EACH, slots)
+        each = min(max(EACH, 8 // groups), slots)
         chunks = slots // each
         blocks = min(BLOCKS, groups)
         mid = extent // 2
@@ -585,9 +585,9 @@
     return on_device
 
 
-EACH = 2
+EACH = 1
 BLOCKS = 8
-LEAD = 2
+LEAD = 4
 
 
 def solution(mesh):

time: 213 us -> 209 us (0.981)
  Pallas kernels: 210 us -> 206 us
    pallas_call x1, Pallas kernels: 210 us -> 206 us  [on_device(): pl.pallas_call(lambda *refs: fused_kernel(sizes, *refs), in_specs=[any_sp...]
where the time goes in v4:
time: 209 us
  Pallas kernels  206 us (99%)
  local copies, waits for them, and re-layouts  3.13 us (1%)
    pallas_call x1, Pallas kernels, on_device(): pl.pallas_call(lambda *refs: fused_kernel(sizes, *refs), in_specs=[any_sp...  206 us

profile of v4, /device:TPU:9, one launch (start us, length us, event | category | flops | bytes accessed | tf_op | source)
XLA Modules:
  0.0 209.1 jit_solution(6060414141368365393)
XLA Ops:
  0.0 205.9 %fused.1 = f32[2048,256]{1,0:T(8,128)} custom-call(f32[2048,256]{1,0:T(8,128)} %bitcast.4, f32[2048,256]{1,0:T(8,128)} %bitcast.5, bf16[2,256,512]{2,1,0:T(8,128)(2,1)} %constant.10.clone.refs_2_, bf16[2,512,256]{2,1,0:T(8,128)(2,1)} %constant.11.clone.refs_3_, bf16[2,2,256,256]{3,2,1,0:T(8,128)(2,1)} %constant.15.refs_4_, ...), custom_call_target="tpu_custom_call" | custom-call | tf_op jit(solution)/shard_map/fused/pallas_call | solution.py:546
  205.9 3.1 %copy.9 = f32[32,64,256]{2,1,0:T(8,128)} copy(f32[32,64,256]{2,1,0:T(8,128)} %bitcast.3) | data formatting | bytes 4194304

commit v5 on v4

--- a/solution.py
+++ b/solution.py
@@ -40,7 +40,7 @@
 
 def fused_kernel(sizes, dens_hbm, green_hbm, f_hbm, ft_hbm, w_hbm, wt_hbm, fold_hbm, out_hbm,
                  dens_in, green_in, f_ref, ft_ref, w_ref, wt_ref, fold_ref, out_ref,
-                 dens_two, green_two, raw_out, raw_in, far_two, dsend, drecv, gsend, grecv,
+                 dens_two, green_two, raw_out, raw_in, dsend, drecv, gsend, grecv,
                  bsend, brecv, ret_out, ret_in, total, in_sem, dens_sem, out_sem, raw_ssem,
                  raw_rsem, d_ssem, d_rsem, g_ssem, g_rsem, b_ssem, b_rsem, ret_ssem, ret_rsem, n_ssem, n_rsem,
                  o_rsem):
@@ -154,13 +154,15 @@
             raw_ssem.at[b], raw_rsem.at[spot, b], (row, hc - 1 + away),
         ).start()
 
-    def transform(two, table, send, line):
+    def transform(two, table, send, first):
+        count = table[0].shape[0]
+
         def tile(t, carry):
             start = pl.multiple_of(t * 256, 256)
             right = (two[0, pl.ds(start, 256), :], two[1, pl.ds(start, 256), :])
             result = dot3(table, right, ((1,), (1,)))
             for i in range(2):
-                send[pl.ds(line * extent * groups + t * 2 + i, extent, stride=groups), :] = (
+                send[pl.ds(first * groups + t * 2 + i, count, stride=groups), :] = (
                     result[:, i * 128 : (i + 1) * 128]
                 )
             return carry
@@ -168,9 +170,8 @@
         lax.fori_loop(0, cells // 256, tile, 0)
 
     copies[1].wait()
-    transform(dens_two, (w_ref[half, 0], w_ref[half, 1]), dsend, 0)
-
-    def scatter_dens(lines_sets):
+
+    def scatter_dens(lines_sets, begin, end):
         def one_chunk(chunk, outer):
             def one(step, carry):
                 target = lax.rem(rank + step, team)
@@ -192,9 +193,14 @@
                 )[...]
             return outer
 
-        lax.fori_loop(0, chunks, one_chunk, 0)
-
-    scatter_dens([(0, me)])
+        lax.fori_loop(begin, end, one_chunk, 0)
+
+    stages = 2 if chunks % 2 == 0 else 1
+    stage = extent // stages
+    for i in range(stages):
+        w_part = tuple(w_ref[half, j, i * stage : (i + 1) * stage, :] for j in range(2))
+        transform(dens_two, w_part, dsend, i * stage)
+        scatter_dens([(0, me)], i * chunks // stages, (i + 1) * chunks // stages)
 
     def weigh(g, carry):
         cell = lax.broadcasted_iota(jnp.int32, (128, extent), 0)
@@ -299,16 +305,22 @@
 
     @pl.when(relay_here)
     def _():
-        for t in range(hc):
-            for b in range(blocks):
+        w_far = (w_ref[half, 0, :, 0:mid], w_ref[half, 1, :, 0:mid])
+
+        def far_lines(b, carry):
+            for t in range(hc):
                 view = rows(raw_in.at[t], b * brows, brows)
                 pltpu.make_async_copy(view, view, raw_rsem.at[t, b]).wait()
-                high, low = split(view[...])
-                far_two[0, pl.ds(b * brows, brows), :] = high
-                far_two[1, pl.ds(b * brows, brows), :] = low
-            w_far = (w_ref[half, 0, :, 0:mid], w_ref[half, 1, :, 0:mid])
-            transform(far_two, w_far, dsend, 1 + t)
-        scatter_dens([(1 + t, row * ncol + away * hc + t) for t in range(hc)])
+                result = dot3(w_far, split(view[...]), ((1,), (1,)))
+                for i in range(bgroups):
+                    start = (1 + t) * extent * groups + b * bgroups + i
+                    dsend[pl.ds(start, extent, stride=groups), :] = (
+                        result[:, i * 128 : (i + 1) * 128]
+                    )
+            return carry
+
+        lax.fori_loop(0, blocks, far_lines, 0)
+        scatter_dens([(1 + t, row * ncol + away * hc + t) for t in range(hc)], 0, chunks)
 
     pace(0)
 
@@ -449,6 +461,28 @@
 
     lax.fori_loop(0, groups, near_group, 0)
 
+    for b in range(blocks):
+        wait(raw_out, brows, raw_ssem.at[b])
+
+    wait(brecv, (team - 1) * chunks * size, n_ssem.at[0])
+
+    def drain(chunk, carry):
+        @pl.when(relay_here)
+        def _():
+            wait(drecv, (nsets - 1 + outer) * size, g_ssem.at[chunk])
+            wait(dsend, (1 + hc) * (team - 1) * size, d_ssem.at[chunk])
+            wait(bsend, hc * (nrow - 1) * size, b_ssem.at[chunk])
+
+        @pl.when(jnp.logical_not(relay_here))
+        def _():
+            wait(drecv, (nsets - 1 - nrow) * size, g_ssem.at[chunk])
+            wait(dsend, (team - 1) * size, d_ssem.at[chunk])
+            wait(bsend, hc * nrow * size, b_ssem.at[chunk])
+
+        return carry
+
+    lax.fori_loop(0, chunks, drain, 0)
+
     out_copies = [
         [
             pltpu.make_async_copy(strip(out_ref, b, h), strip(out_hbm, b, h), out_sem.at[b, h])
@@ -474,32 +508,11 @@
         for copy in out_copies[b]:
             copy.start()
 
-    for b in range(blocks):
-        wait(raw_out, brows, raw_ssem.at[b])
-
-    wait(brecv, (team - 1) * chunks * size, n_ssem.at[0])
-
     @pl.when(relay_here)
     def _():
         for b in range(blocks):
             wait(raw_out, hc * bgroups * mid, ret_ssem.at[b])
 
-    def drain(chunk, carry):
-        @pl.when(relay_here)
-        def _():
-            wait(drecv, (nsets - 1 + outer) * size, g_ssem.at[chunk])
-            wait(dsend, (1 + hc) * (team - 1) * size, d_ssem.at[chunk])
-            wait(bsend, hc * (nrow - 1) * size, b_ssem.at[chunk])
-
-        @pl.when(jnp.logical_not(relay_here))
-        def _():
-            wait(drecv, (nsets - 1 - nrow) * size, g_ssem.at[chunk])
-            wait(dsend, (team - 1) * size, d_ssem.at[chunk])
-            wait(bsend, hc * nrow * size, b_ssem.at[chunk])
-
-        return carry
-
-    lax.fori_loop(0, chunks, drain, 0)
     for b in range(blocks):
         for copy in out_copies[b]:
             copy.wait()
@@ -555,7 +568,6 @@
                 pltpu.VMEM((2, cells, extent), BF16),
                 pltpu.VMEM((cells, mid), F32),
                 pltpu.VMEM((hc, cells, mid), F32),
-                pltpu.VMEM((2, cells, mid), BF16),
                 pltpu.VMEM(((1 + hc) * lot, 128), F32),
                 pltpu.VMEM((2 * lot, 128), F32),
                 pltpu.VMEM((lot, 128), F32),

time: 209 us -> 209 us (level)
  no operation moved by 1% of the time
where the time goes in v5:
time: 209 us
  Pallas kernels  205 us (98%)
  local copies, waits for them, and re-layouts  3.13 us (1%)
    pallas_call x1, Pallas kernels, on_device(): pl.pallas_call(lambda *refs: fused_kernel(sizes, *refs), in_specs=[any_sp...  205 us

profile of v5, /device:TPU:9, one launch (start us, length us, event | category | flops | bytes accessed | tf_op | source)
XLA Modules:
  0.0 208.6 jit_solution(1545490178770286687)
XLA Ops:
  0.0 205.5 %fused.1 = f32[2048,256]{1,0:T(8,128)} custom-call(f32[2048,256]{1,0:T(8,128)} %bitcast.4, f32[2048,256]{1,0:T(8,128)} %bitcast.5, bf16[2,256,512]{2,1,0:T(8,128)(2,1)} %constant.10.clone.refs_2_, bf16[2,512,256]{2,1,0:T(8,128)(2,1)} %constant.11.clone.refs_3_, bf16[2,2,256,256]{3,2,1,0:T(8,128)(2,1)} %constant.15.refs_4_, ...), custom_call_target="tpu_custom_call" | custom-call | tf_op jit(solution)/shard_map/fused/pallas_call | solution.py:559
  205.5 3.1 %copy.9 = f32[32,64,256]{2,1,0:T(8,128)} copy(f32[32,64,256]{2,1,0:T(8,128)} %bitcast.3) | data formatting | bytes 4194304
